TPU v7x, 128 devices: a whole 4x4x4 slice. The times are simulated.
128 devices in a mesh: node: 64 (over z, y, x), hand: 2 (over core).
Axes of the slice: x: 4, y: 4, z: 4, core: 2. Of those that a mesh axis runs over, the one named last changes fastest.
Arguments:
- ranges: bfloat16 [2048, 128, 1326], P('node', None, 'hand'), may hold values from 0.00019931793 to 0.0039978027
- strengths: int32 [2048, 1326], P('node'), may hold values from 0 to 399
- live_hands: int32 [2048, 1326], P('node'), may hold values 0 or 1
- pot_sizes: float32 [2048, 128], P('node'), may hold values from 1 to 16
- action_counts: int32 [2048], P('node'), may hold values from 1 to 8
- parents: int32 [2048], P('node'), may hold values from 0 to 255
- turn_counts: int32 [64], replicated, may hold values from 1 to 4
- root_reach: float32 [64, 2, 1326], P(None, None, 'hand'), may hold values from 0.01 to 1
Outputs:
- turn_values: float32 [64, 2, 1326], P('node', None, 'hand')
- exploitability: float32 [], replicated
All inputs are finite; a program needn't handle non-finite values. No bound on the sum of `live_hands` on one device may be relied on, other than what follows from the above.
Results may differ from a plain program's by a relative error of at most 0.0003.
Values may be sent and summed in bfloat16 or wider, within the bound.
A program may use at most 128 MiB of HBM per device.

v0:
```python
import functools
import jax
import jax.numpy as jnp
import numpy as np
from jax import lax
from jax.sharding import Mesh
from jax.sharding import PartitionSpec as P

ACT = 8
GROUPS = 8
TACT = 4
NODE = ("node_0", "node_1", "node_2")
NODE_HAND = ("node_0", "node_1", "node_2", "hand")


def cut_along(shard, dim, count):
    before, after = (shard.shape[:dim], shard.shape[dim + 1 :])
    return jnp.moveaxis(shard.reshape(*before, count, -1, *after), dim, 0)


def sent_and_summed(shard, axis, dim):
    count = lax.axis_size(axis)
    parts = lax.all_to_all(cut_along(shard, dim, count), axis, 0, 0, tiled=True)
    return jnp.sum(parts, axis=0)


def one_axis_at_a_time(shard, axes):
    return functools.reduce(lax.psum, axes, shard)


def card_pairs(wanted):
    first_list = []
    second_list = []
    for lower_card in range(52):
        for upper_card in range(lower_card + 1, 52):
            first_list.append(lower_card)
            second_list.append(upper_card)
    return (
        jnp.asarray(np.array(first_list[:wanted], dtype=np.int32)),
        jnp.asarray(np.array(second_list[:wanted], dtype=np.int32)),
    )


def pair_compat(row_first, row_second, col_first, col_second):
    shared = (row_first[:, None] == col_first[None, :]) | (
        row_first[:, None] == col_second[None, :]
    )
    shared = (
        shared
        | (row_second[:, None] == col_first[None, :])
        | (row_second[:, None] == col_second[None, :])
    )
    return jnp.where(shared, 0.0, 1.0).astype(jnp.float32)


def showdown_block(compat, packed):
    left_strength, left_live, right_strength, right_live, reach_block = packed
    signs = jnp.sign((left_strength[:, :, None] - right_strength[:, None, :]).astype(jnp.float32))
    matrix = (signs * compat[None] * left_live[:, :, None] * right_live[:, None, :]).astype(
        jnp.bfloat16
    )
    return jnp.einsum("nij,nlj->nli", matrix, reach_block, preferred_element_type=jnp.float32)


def river_from(raw_values, pots, legal):
    count = raw_values.shape[0]
    width = raw_values.shape[2]
    values = (raw_values * pots[:, :, None]).reshape(count, 2, GROUPS, ACT, width)
    usable = jnp.arange(ACT)[None, :] < legal[:, None]
    return jnp.where(usable[:, None, None, :, None], values, -1e30).max(axis=3).sum(axis=2)


def turn_best(sums, legal):
    hand_half = sums.shape[1] // 2
    shaped = sums.reshape(-1, TACT, 2, hand_half)
    usable = jnp.arange(TACT)[None, :] < legal[:, None]
    return jnp.where(usable[:, :, None, None], shaped, -1e30).max(axis=1)


def local(
    ranges, strengths, live_hands, pot_sizes, action_counts, parents, turn_counts, root_reach
):
    node_count, line_cols, hand_half = ranges.shape
    hands_all = strengths.shape[1]
    hand_start = lax.axis_index("hand") * hand_half
    first_card, second_card = card_pairs(hands_all)
    live_all = live_hands.astype(jnp.float32)
    blocks = node_count // 4

    def grouped(array):
        return array.reshape((blocks, 4) + array.shape[1:])

    row_first = lax.dynamic_slice_in_dim(first_card, hand_start, hand_half, 0)
    row_second = lax.dynamic_slice_in_dim(second_card, hand_start, hand_half, 0)
    row_strength = lax.dynamic_slice_in_dim(strengths, hand_start, hand_half, 1)
    row_live = lax.dynamic_slice_in_dim(live_all, hand_start, hand_half, 1)
    compat = pair_compat(row_first, row_second, first_card, second_card)

    def one_block(packed):
        return showdown_block(compat, packed)

    added = lax.map(
        one_block,
        (
            grouped(row_strength),
            grouped(row_live),
            grouped(strengths),
            grouped(live_all),
            grouped(lax.all_gather(ranges, "hand", axis=2, tiled=True)),
        ),
    )
    raw_values = added.reshape(jnp.zeros((node_count, line_cols, hand_half), jnp.float32).shape)
    river_best = river_from(raw_values, pot_sizes, action_counts)
    flat_best = river_best.reshape(node_count, 2 * hand_half)
    turns_all = turn_counts.shape[0]
    turns_mine = turns_all // lax.axis_size(NODE)
    turn_start = lax.axis_index(NODE) * turns_mine
    rows_mine = turns_mine * TACT
    targets = jnp.arange(rows_mine * lax.axis_size(NODE), dtype=jnp.int32)
    onehot = (parents[None, :] == targets[:, None]).astype(jnp.float32)
    mine = sent_and_summed(jnp.dot(onehot, flat_best, precision=lax.Precision.HIGHEST), NODE, 0)
    legal_mine = lax.dynamic_slice_in_dim(turn_counts, turn_start, turns_mine, 0)
    turn_values = turn_best(mine, legal_mine)
    reach_mine = lax.dynamic_slice_in_dim(root_reach, turn_start, turns_mine, 0)
    exploitability = one_axis_at_a_time(jnp.sum(reach_mine * turn_values), NODE_HAND)
    return (turn_values, exploitability)


def solution(mesh):
    split = Mesh(
        mesh.devices.reshape(4, 4, 4, mesh.shape["hand"]), ("node_0", "node_1", "node_2", "hand")
    )
    in_specs = (
        P(NODE, None, "hand"),
        P(NODE, None),
        P(NODE, None),
        P(NODE, None),
        P(NODE),
        P(NODE),
        P(),
        P(None, None, "hand"),
    )
    out_specs = (P(NODE, None, "hand"), P())
    return jax.shard_map(local, mesh=split, in_specs=in_specs, out_specs=out_specs, check_vma=False)
```

profile of v0, /device:TPU:1, one launch (start us, length us, event | category | flops | bytes accessed | tf_op | source)
XLA Modules:
  0.0 228.3 jit_solution(14435566055462864649)
XLA Ops:
  7.2 0.7 all-gather.2.cloned.1.call-update
  8.0 0.9 convert_element_type.10
  9.1 1.0 reshape.101
  10.1 1.0 constant_dynamic-slice_fusion.2
  11.1 0.8 dynamic_slice.40
  11.9 0.8 dynamic_slice.41
  12.7 0.8 copy.24
  13.7 25.3 %all-gather.2.cloned.1.call-done = bf16[32,128,1326]{1,0,2:T(8,128)(2,1)} async-done(((bf16[32,128,663]{1,0,2:T(8,128)(2,1)}), bf16[32,128,1326]{1,0,2:T(8,128)(2,1)}) %all-gather.2.cloned.1.call-update) | async-done | bytes 10862608 | tf_op jit(solution)/shard_map/all_gather | solution.py:109
  39.1 84.1 %while.11 = (s32[]{:T(128)}, f32[8,4,128,663]{2,3,1,0:T(8,128)}, bf16[8,4,128,1326]{2,1,0,3:T(4,128)(2,1)}, s32[8,4,663]{2,1,0:T(4,128)S(1)}, s32[8,4,1326]{2,1,...) while((s32[]{:T(128)}, f32[8,4,128,663]{2,3,1,0:T(8,128)}, ...), condition=%wide.region_1.2_spmd.clone, body=%wide.region_0.1_spmd.clone.sunk | while | flops 931886272 | bytes 12673953 | solution.py:102
  39.1 1.6 constant_dynamic-slice_fusion.4
  40.7 1.5 or_select_fusion.2
  42.3 7.3 %fusion.11 = f32[8,4,128,663]{2,3,1,0:T(8,128)} fusion(f32[8,4,128,663]{2,3,1,0:T(8,128)} %get-tuple-element.197, s32[]{:T(128)} %get-tuple-element.196, f32[4,1326]{1,0:T(4,128)S(1)} %dynamic-slice_bitcast_fusion.8, f32[4,663]{1,0:T(4,128)S(1)} %dynamic-slice_bitcast_fusion.9, f32[663,1326]{1,0:T(8,128)S(1)} %or_select_fusion.2, ...), kind=kOutput, calls=%fused_computation.5.clone.1 | convolution fusion | flops 924853184 | bytes 6298408 | tf_op jit(solution)/shard_map/while/body/eval_jaxpr/nij,nlj->nli/dot_general | solution.py:62
  49.6 1.6 constant_dynamic-slice_fusion.4
  51.3 1.5 or_select_fusion.2
  52.8 7.3 %fusion.11 = f32[8,4,128,663]{2,3,1,0:T(8,128)} fusion(f32[8,4,128,663]{2,3,1,0:T(8,128)} %get-tuple-element.197, s32[]{:T(128)} %get-tuple-element.196, f32[4,1326]{1,0:T(4,128)S(1)} %dynamic-slice_bitcast_fusion.8, f32[4,663]{1,0:T(4,128)S(1)} %dynamic-slice_bitcast_fusion.9, f32[663,1326]{1,0:T(8,128)S(1)} %or_select_fusion.2, ...), kind=kOutput, calls=%fused_computation.5.clone.1 | convolution fusion | flops 924853184 | bytes 6298408 | tf_op jit(solution)/shard_map/while/body/eval_jaxpr/nij,nlj->nli/dot_general | solution.py:62
  60.1 1.6 constant_dynamic-slice_fusion.4
  61.8 1.5 or_select_fusion.2
  63.3 7.3 %fusion.11 = f32[8,4,128,663]{2,3,1,0:T(8,128)} fusion(f32[8,4,128,663]{2,3,1,0:T(8,128)} %get-tuple-element.197, s32[]{:T(128)} %get-tuple-element.196, f32[4,1326]{1,0:T(4,128)S(1)} %dynamic-slice_bitcast_fusion.8, f32[4,663]{1,0:T(4,128)S(1)} %dynamic-slice_bitcast_fusion.9, f32[663,1326]{1,0:T(8,128)S(1)} %or_select_fusion.2, ...), kind=kOutput, calls=%fused_computation.5.clone.1 | convolution fusion | flops 924853184 | bytes 6298408 | tf_op jit(solution)/shard_map/while/body/eval_jaxpr/nij,nlj->nli/dot_general | solution.py:62
  70.6 1.6 constant_dynamic-slice_fusion.4
  72.3 1.5 or_select_fusion.2
  73.9 7.3 %fusion.11 = f32[8,4,128,663]{2,3,1,0:T(8,128)} fusion(f32[8,4,128,663]{2,3,1,0:T(8,128)} %get-tuple-element.197, s32[]{:T(128)} %get-tuple-element.196, f32[4,1326]{1,0:T(4,128)S(1)} %dynamic-slice_bitcast_fusion.8, f32[4,663]{1,0:T(4,128)S(1)} %dynamic-slice_bitcast_fusion.9, f32[663,1326]{1,0:T(8,128)S(1)} %or_select_fusion.2, ...), kind=kOutput, calls=%fused_computation.5.clone.1 | convolution fusion | flops 924853184 | bytes 6298408 | tf_op jit(solution)/shard_map/while/body/eval_jaxpr/nij,nlj->nli/dot_general | solution.py:62
  81.1 1.6 constant_dynamic-slice_fusion.4
  82.8 1.5 or_select_fusion.2
  84.3 7.3 %fusion.11 = f32[8,4,128,663]{2,3,1,0:T(8,128)} fusion(f32[8,4,128,663]{2,3,1,0:T(8,128)} %get-tuple-element.197, s32[]{:T(128)} %get-tuple-element.196, f32[4,1326]{1,0:T(4,128)S(1)} %dynamic-slice_bitcast_fusion.8, f32[4,663]{1,0:T(4,128)S(1)} %dynamic-slice_bitcast_fusion.9, f32[663,1326]{1,0:T(8,128)S(1)} %or_select_fusion.2, ...), kind=kOutput, calls=%fused_computation.5.clone.1 | convolution fusion | flops 924853184 | bytes 6298408 | tf_op jit(solution)/shard_map/while/body/eval_jaxpr/nij,nlj->nli/dot_general | solution.py:62
  91.7 1.6 constant_dynamic-slice_fusion.4
  93.3 1.5 or_select_fusion.2
  94.9 7.3 %fusion.11 = f32[8,4,128,663]{2,3,1,0:T(8,128)} fusion(f32[8,4,128,663]{2,3,1,0:T(8,128)} %get-tuple-element.197, s32[]{:T(128)} %get-tuple-element.196, f32[4,1326]{1,0:T(4,128)S(1)} %dynamic-slice_bitcast_fusion.8, f32[4,663]{1,0:T(4,128)S(1)} %dynamic-slice_bitcast_fusion.9, f32[663,1326]{1,0:T(8,128)S(1)} %or_select_fusion.2, ...), kind=kOutput, calls=%fused_computation.5.clone.1 | convolution fusion | flops 924853184 | bytes 6298408 | tf_op jit(solution)/shard_map/while/body/eval_jaxpr/nij,nlj->nli/dot_general | solution.py:62
  102.2 1.6 constant_dynamic-slice_fusion.4
  103.9 1.5 or_select_fusion.2
  105.4 7.3 %fusion.11 = f32[8,4,128,663]{2,3,1,0:T(8,128)} fusion(f32[8,4,128,663]{2,3,1,0:T(8,128)} %get-tuple-element.197, s32[]{:T(128)} %get-tuple-element.196, f32[4,1326]{1,0:T(4,128)S(1)} %dynamic-slice_bitcast_fusion.8, f32[4,663]{1,0:T(4,128)S(1)} %dynamic-slice_bitcast_fusion.9, f32[663,1326]{1,0:T(8,128)S(1)} %or_select_fusion.2, ...), kind=kOutput, calls=%fused_computation.5.clone.1 | convolution fusion | flops 924853184 | bytes 6298408 | tf_op jit(solution)/shard_map/while/body/eval_jaxpr/nij,nlj->nli/dot_general | solution.py:62
  112.7 1.6 constant_dynamic-slice_fusion.4
  114.3 1.5 or_select_fusion.2
  115.9 7.3 %fusion.11 = f32[8,4,128,663]{2,3,1,0:T(8,128)} fusion(f32[8,4,128,663]{2,3,1,0:T(8,128)} %get-tuple-element.197, s32[]{:T(128)} %get-tuple-element.196, f32[4,1326]{1,0:T(4,128)S(1)} %dynamic-slice_bitcast_fusion.8, f32[4,663]{1,0:T(4,128)S(1)} %dynamic-slice_bitcast_fusion.9, f32[663,1326]{1,0:T(8,128)S(1)} %or_select_fusion.2, ...), kind=kOutput, calls=%fused_computation.5.clone.1 | convolution fusion | flops 924853184 | bytes 6298408 | tf_op jit(solution)/shard_map/while/body/eval_jaxpr/nij,nlj->nli/dot_general | solution.py:62
  123.2 12.0 %copy.23 = f32[8,4,128,663]{3,2,1,0:T(8,128)} copy(f32[8,4,128,663]{2,3,1,0:T(8,128)} %get-tuple-element.44) | data formatting | bytes 21725184 | tf_op jit(solution)/shard_map/while | solution.py:102
  135.1 16.8 %select_reduce_fusion = f32[32,2,8,663]{3,2,1,0:T(8,128)S(1)} fusion(f32[32,2,8,8,663]{4,3,2,1,0:T(8,128)} %bitcast.32, f32[32,2,8,8]{3,2,1,0:T(8,128)S(1)} %copy.25, pred[32,8]{1,0:T(8,128)(4,1)S(1)} %iota_compare_fusion), kind=kLoop, calls=%fused_computation.12 | loop fusion | flops 7807488 | bytes 12237056 | tf_op jit(solution)/shard_map/reduce_max | solution.py:70
  152.0 0.5 reduce_sum.27
  152.6 0.8 fusion.5
  153.5 2.0 copy.26
  155.5 10.1 %all-to-all-start = ((f32[64,4,1326]{2,1,0:T(4,128)}), f32[64,4,1326]{2,1,0:T(4,128)S(1)}, u32[]{:S(2)}, u32[]{:S(2)}) async-start(f32[64,4,1326]{2,1,0:T(4,128)} %copy.26), calls=%async_computation | async-start | bytes 2883584 | tf_op jit(solution)/shard_map/all_to_all | solution.py:23
  165.7 0.6 dynamic_slice.38
  166.3 0.6 iota_compare_fusion.1
  166.9 21.1 %all-to-all-done = f32[64,4,1326]{2,1,0:T(4,128)S(1)} async-done(((f32[64,4,1326]{2,1,0:T(4,128)}), f32[64,4,1326]{2,1,0:T(4,128)S(1)}, u32[]{:S(2)}, u32[]{:S(2)}) %all-to-all-start) | async-done | bytes 1357856 | tf_op jit(solution)/shard_map/all_to_all | solution.py:23
  188.0 0.3 reduce_sum.28
  188.5 1.3 multiply_reduce_fusion
  189.8 7.1 %psum.28 = f32[]{:T(128)} all-reduce(f32[]{:T(128)} %multiply_reduce_fusion), channel_id=1, replica_groups=mesh['node_0'=4,'node_1'=4,'node_2'=4,'hand'=2] {'node_0'}, use_global_device_ids=true, to_apply=%region_7.8 | all-reduce | flops 1 | bytes 8 | tf_op jit(solution)/shard_map/psum | solution.py:28
  196.9 7.5 %psum.29 = f32[]{:T(128)} all-reduce(f32[]{:T(128)} %psum.28), channel_id=1, replica_groups=mesh['node_0'=4,'node_1'=4,'node_2'=4,'hand'=2] {'node_1'}, use_global_device_ids=true, to_apply=%region_8.9 | all-reduce | flops 1 | bytes 8 | tf_op jit(solution)/shard_map/psum | solution.py:28
  204.4 6.9 %psum.30 = f32[]{:T(128)} all-reduce(f32[]{:T(128)} %psum.29), channel_id=1, replica_groups=mesh['node_0'=4,'node_1'=4,'node_2'=4,'hand'=2] {'node_2'}, use_global_device_ids=true, to_apply=%region_9.10 | all-reduce | flops 1 | bytes 8 | tf_op jit(solution)/shard_map/psum | solution.py:28
  211.3 10.2 %psum.31 = f32[]{:T(128)} all-reduce(f32[]{:T(128)} %psum.30), channel_id=1, replica_groups=mesh['node_0'=4,'node_1'=4,'node_2'=4,'hand'=2] {'hand'}, use_global_device_ids=true, to_apply=%region_10.11 | all-reduce | flops 1 | bytes 8 | tf_op jit(solution)/shard_map/psum | solution.py:28
  (56 shorter events, 1.2 us)
Async XLA Ops:
  7.2 31.9 %copy-start = (s32[1326]{0:T(1024)S(1)}, s32[1326]{0:T(1024)}, u32[]{:S(2)}) copy-start(s32[1326]{0:T(1024)} %constant.58.clone) | copy-start | bytes 15916
  7.2 31.9 %copy-start.1 = (s32[1326]{0:T(1024)S(1)}, s32[1326]{0:T(1024)}, u32[]{:S(2)}) copy-start(s32[1326]{0:T(1024)} %constant.59.clone) | copy-start | bytes 15916
  7.2 6.5 %copy-start.4 = (s32[32]{0:T(128)S(1)}, s32[32]{0:T(128)}, u32[]{:S(2)}) copy-start(s32[32]{0:T(128)} %param.16) | copy-start | bytes 388
  7.2 31.9 %all-gather.2.cloned.1.call-start = ((), (), s32[]{:S(2)}) async-start(), calls=%async_computation.1 | async-start | bytes 16293888 | tf_op jit(solution)/shard_map/all_gather | solution.py:109
  135.1 17.5 %copy-start.3 = (s32[32]{0:T(128)S(1)}, s32[32]{0:T(128)}, u32[]{:S(2)}) copy-start(s32[32]{0:T(128)} %param.17) | copy-start | bytes 388
  152.0 13.7 %copy-start.5 = (s32[64]{0:T(128)S(1)}, s32[64]{0:T(128)}, u32[]{:S(2)}) copy-start(s32[64]{0:T(128)} %param.18) | copy-start | bytes 772
  155.5 32.5 %all-to-all-start = ((f32[64,4,1326]{2,1,0:T(4,128)}), f32[64,4,1326]{2,1,0:T(4,128)S(1)}, u32[]{:S(2)}, u32[]{:S(2)}) async-start(f32[64,4,1326]{2,1,0:T(4,128)} %copy.26), calls=%async_computation | async-start | bytes 2883584 | tf_op jit(solution)/shard_map/all_to_all | solution.py:23
  188.5 33.0 %copy-start.2 = (f32[1,2,663]{2,1,0:T(2,128)}, f32[1,2,663]{2,1,0:T(2,128)S(1)}, u32[]{:S(2)}) copy-start(f32[1,2,663]{2,1,0:T(2,128)S(1)} %reduce_max.22) | copy-start | bytes 15916
Sparse Core Ops, SparseCore 0:
  9.7 29.3 all-gather.1
where the time goes:
time: 229 us; the launch traced here: 228 us
  matrix products  59.2 us (26%)
  waiting for transfers between devices  47.1 us (21%)
  other arithmetic  32.8 us (14%)
  local copies, waits for them, and re-layouts  32.7 us (14%)
  blocking collectives  31.7 us (14%)
  between operations  14.2 us (6%)
  starting transfers between devices  10.2 us (4%)
    dot_general x8, matrix products, showdown_block(): jnp.einsum('nij,nlj->nli', matrix, reach_block, preferred_element_type=jn...  58.4 us
    psum x4, blocking collectives, one_axis_at_a_time(): return functools.reduce(lax.psum, axes, shard)  31.7 us
    all_gather x1, waiting for transfers between devices, local(): lax.all_gather(ranges, 'hand', axis=2, tiled=True)  25.3 us
    all_to_all x1, waiting for transfers between devices, sent_and_summed(): parts = lax.all_to_all(cut_along(shard, dim, count), axis, 0, 0, tiled=True)  21.1 us
    reduce_max x1, other arithmetic, river_from(): jnp.where(usable[:, None, None, :, None], values, -1e+30).max(axis=3)  16.8 us
    dynamic_slice x8, local copies, waits for them, and re-layouts, local(): lax.map(one_block, (grouped(row_strength), grouped(row_live), grouped(str...  12.8 us
    select_n x8, other arithmetic, pair_compat(): return jnp.where(shared, 0.0, 1.0).astype(jnp.float32)  12.2 us
    while x1, local copies, waits for them, and re-layouts, local(): lax.map(one_block, (grouped(row_strength), grouped(row_live), grouped(str...  12 us
  transfers between devices with their start and end apart: 2, of which 2 were waited for; matrix products, arithmetic and copies ran while one was open for 3% of the time, Pallas kernels for 0%

commit v1 on v0

--- a/solution.py
+++ b/solution.py
@@ -11,6 +11,19 @@
 TACT = 4
 NODE = ("node_0", "node_1", "node_2")
 NODE_HAND = ("node_0", "node_1", "node_2", "hand")
+
+
+def _post_sites(arr, in_dim):
+    e_next = jnp.concatenate(
+        lax.all_to_all(
+            jnp.stack(tuple((arr for _ in range(lax.axis_size("hand")))), axis=0), "hand", 0, 0
+        ),
+        in_dim,
+    )
+    return e_next
+
+
+unite_lots_all = functools.partial(_post_sites, in_dim=2)
 
 
 def cut_along(shard, dim, count):
@@ -106,7 +119,7 @@
             grouped(row_live),
             grouped(strengths),
             grouped(live_all),
-            grouped(lax.all_gather(ranges, "hand", axis=2, tiled=True)),
+            grouped(unite_lots_all(ranges)),
         ),
     )
     raw_values = added.reshape(jnp.zeros((node_count, line_cols, hand_half), jnp.float32).shape)

time: 229 us -> 214 us (0.934)
  waiting for transfers between devices: 47.1 us -> 29.3 us
  between operations: 14.2 us -> 0.8 us
  starting transfers between devices: 10.2 us -> 20.5 us
  other arithmetic: 32.8 us -> 42.5 us
  local copies, waits for them, and re-layouts: 32.7 us -> 28.9 us
    all_gather x1 -> x0, waiting for transfers between devices: 25.3 us -> none  [local(): lax.all_gather(ranges, 'hand', axis=2, tiled=True)]
    another operation x0 -> x1, other arithmetic: none -> 10.6 us  [_post_sites(): jnp.stack(tuple((arr for _ in range(lax.axis_size('hand')))), axis=0)]
    all_to_all x0 -> x1, starting transfers between devices: none -> 9.3 us  [_post_sites(): lax.all_to_all(jnp.stack(tuple((arr for _ in range(lax.axis_size('hand'))...]
    all_to_all x0 -> x1, waiting for transfers between devices: none -> 8.28 us  [_post_sites(): lax.all_to_all(jnp.stack(tuple((arr for _ in range(lax.axis_size('hand'))...]
  transfers between devices with their start and end apart: 2 -> 2, of which waited for: 2 -> 2; matrix products, arithmetic and copies ran while one was open for 3% -> 1% of each run, Pallas kernels for 0% -> 0%
where the time goes in v1:
time: 214 us; the launch traced here: 213 us
  matrix products  59.2 us (28%)
  other arithmetic  42.5 us (20%)
  blocking collectives  31.8 us (15%)
  waiting for transfers between devices  29.3 us (14%)
  local copies, waits for them, and re-layouts  28.9 us (14%)
  starting transfers between devices  20.5 us (10%)
    dot_general x8, matrix products, showdown_block(): jnp.einsum('nij,nlj->nli', matrix, reach_block, preferred_element_type=jn...  58.4 us
    psum x4, blocking collectives, one_axis_at_a_time(): return functools.reduce(lax.psum, axes, shard)  31.8 us
    all_to_all x1, waiting for transfers between devices, sent_and_summed(): parts = lax.all_to_all(cut_along(shard, dim, count), axis, 0, 0, tiled=True)  21 us
    reduce_max x1, other arithmetic, river_from(): jnp.where(usable[:, None, None, :, None], values, -1e+30).max(axis=3)  16.8 us
    dynamic_slice x8, local copies, waits for them, and re-layouts, local(): lax.map(one_block, (grouped(row_strength), grouped(row_live), grouped(str...  12.8 us
    select_n x8, other arithmetic, pair_compat(): return jnp.where(shared, 0.0, 1.0).astype(jnp.float32)  12.2 us
    while x1, local copies, waits for them, and re-layouts, local(): lax.map(one_block, (grouped(row_strength), grouped(row_live), grouped(str...  12 us
    all_to_all x1, starting transfers between devices, sent_and_summed(): parts = lax.all_to_all(cut_along(shard, dim, count), axis, 0, 0, tiled=True)  11.2 us
  transfers between devices with their start and end apart: 2, of which 2 were waited for; matrix products, arithmetic and copies ran while one was open for 1% of the time, Pallas kernels for 0%

profile of v1, /device:TPU:1, one launch (start us, length us, event | category | flops | bytes accessed | tf_op | source)
XLA Modules:
  0.0 213.4 jit_solution(6697935267795248760)
XLA Ops:
  0.6 10.6 %pad_maximum_fusion = bf16[2,32,128,663]{2,1,3,0:T(8,128)(2,1)} fusion(bf16[1,32,128,663]{2,1,3,0:T(8,128)(2,1)} %bitcast.36), kind=kLoop, calls=%fused_computation.13 | loop fusion | flops 5431296 | bytes 16293888 | tf_op jit(solution)/shard_map/stack | solution.py:19
  11.3 9.3 %all-to-all-start = ((bf16[2,32,128,663]{2,1,3,0:T(8,128)(2,1)}), bf16[2,32,128,663]{2,1,3,0:T(8,128)(2,1)}, u32[]{:S(2)}, u32[]{:S(2)}) async-start(bf16[2,32,128,663]{2,1,3,0:T(8,128)(2,1)} %pad_maximum_fusion), calls=%async_computation | async-start | bytes 21725184 | tf_op jit(solution)/shard_map/all_to_all | solution.py:18
  20.6 0.1 constant_dynamic-slice_fusion.1
  20.7 0.1 constant_dynamic-slice_fusion.2
  21.2 8.3 %all-to-all-done = bf16[2,32,128,663]{2,1,3,0:T(8,128)(2,1)} async-done(((bf16[2,32,128,663]{2,1,3,0:T(8,128)(2,1)}), bf16[2,32,128,663]{2,1,3,0:T(8,128)(2,1)}, u32[]{:S(2)}, u32[]{:S(2)}) %all-to-all-start) | async-done | bytes 10862624 | tf_op jit(solution)/shard_map/all_to_all | solution.py:18
  29.4 84.1 %while.11 = (s32[]{:T(128)}, f32[8,4,128,663]{2,3,1,0:T(8,128)}, bf16[8,4,128,1326]{2,1,0,3:T(4,128)(2,1)}, s32[8,4,663]{2,1,0:T(4,128)S(1)}, s32[8,4,1326]{2,1,...) while((s32[]{:T(128)}, f32[8,4,128,663]{2,3,1,0:T(8,128)}, ...), condition=%wide.region_1.2_spmd.clone, body=%wide.region_0.1_spmd.clone.sunk | while | flops 931886272 | bytes 12673953 | solution.py:115
  29.4 1.6 constant_dynamic-slice_fusion.4
  31.1 1.5 or_select_fusion.2
  32.7 7.3 %fusion.11 = f32[8,4,128,663]{2,3,1,0:T(8,128)} fusion(f32[8,4,128,663]{2,3,1,0:T(8,128)} %get-tuple-element.208, s32[]{:T(128)} %get-tuple-element.207, f32[4,1326]{1,0:T(4,128)S(1)} %dynamic-slice_bitcast_fusion.8, f32[4,663]{1,0:T(4,128)S(1)} %dynamic-slice_bitcast_fusion.9, f32[663,1326]{1,0:T(8,128)S(1)} %or_select_fusion.2, ...), kind=kOutput, calls=%fused_computation.5.clone.1 | convolution fusion | flops 924853184 | bytes 6298408 | tf_op jit(solution)/shard_map/while/body/eval_jaxpr/nij,nlj->nli/dot_general | solution.py:75
  39.9 1.6 constant_dynamic-slice_fusion.4
  41.6 1.5 or_select_fusion.2
  43.2 7.3 %fusion.11 = f32[8,4,128,663]{2,3,1,0:T(8,128)} fusion(f32[8,4,128,663]{2,3,1,0:T(8,128)} %get-tuple-element.208, s32[]{:T(128)} %get-tuple-element.207, f32[4,1326]{1,0:T(4,128)S(1)} %dynamic-slice_bitcast_fusion.8, f32[4,663]{1,0:T(4,128)S(1)} %dynamic-slice_bitcast_fusion.9, f32[663,1326]{1,0:T(8,128)S(1)} %or_select_fusion.2, ...), kind=kOutput, calls=%fused_computation.5.clone.1 | convolution fusion | flops 924853184 | bytes 6298408 | tf_op jit(solution)/shard_map/while/body/eval_jaxpr/nij,nlj->nli/dot_general | solution.py:75
  50.5 1.6 constant_dynamic-slice_fusion.4
  52.1 1.5 or_select_fusion.2
  53.7 7.3 %fusion.11 = f32[8,4,128,663]{2,3,1,0:T(8,128)} fusion(f32[8,4,128,663]{2,3,1,0:T(8,128)} %get-tuple-element.208, s32[]{:T(128)} %get-tuple-element.207, f32[4,1326]{1,0:T(4,128)S(1)} %dynamic-slice_bitcast_fusion.8, f32[4,663]{1,0:T(4,128)S(1)} %dynamic-slice_bitcast_fusion.9, f32[663,1326]{1,0:T(8,128)S(1)} %or_select_fusion.2, ...), kind=kOutput, calls=%fused_computation.5.clone.1 | convolution fusion | flops 924853184 | bytes 6298408 | tf_op jit(solution)/shard_map/while/body/eval_jaxpr/nij,nlj->nli/dot_general | solution.py:75
  61.0 1.6 constant_dynamic-slice_fusion.4
  62.6 1.5 or_select_fusion.2
  64.2 7.3 %fusion.11 = f32[8,4,128,663]{2,3,1,0:T(8,128)} fusion(f32[8,4,128,663]{2,3,1,0:T(8,128)} %get-tuple-element.208, s32[]{:T(128)} %get-tuple-element.207, f32[4,1326]{1,0:T(4,128)S(1)} %dynamic-slice_bitcast_fusion.8, f32[4,663]{1,0:T(4,128)S(1)} %dynamic-slice_bitcast_fusion.9, f32[663,1326]{1,0:T(8,128)S(1)} %or_select_fusion.2, ...), kind=kOutput, calls=%fused_computation.5.clone.1 | convolution fusion | flops 924853184 | bytes 6298408 | tf_op jit(solution)/shard_map/while/body/eval_jaxpr/nij,nlj->nli/dot_general | solution.py:75
  71.4 1.6 constant_dynamic-slice_fusion.4
  73.1 1.5 or_select_fusion.2
  74.6 7.3 %fusion.11 = f32[8,4,128,663]{2,3,1,0:T(8,128)} fusion(f32[8,4,128,663]{2,3,1,0:T(8,128)} %get-tuple-element.208, s32[]{:T(128)} %get-tuple-element.207, f32[4,1326]{1,0:T(4,128)S(1)} %dynamic-slice_bitcast_fusion.8, f32[4,663]{1,0:T(4,128)S(1)} %dynamic-slice_bitcast_fusion.9, f32[663,1326]{1,0:T(8,128)S(1)} %or_select_fusion.2, ...), kind=kOutput, calls=%fused_computation.5.clone.1 | convolution fusion | flops 924853184 | bytes 6298408 | tf_op jit(solution)/shard_map/while/body/eval_jaxpr/nij,nlj->nli/dot_general | solution.py:75
  82.0 1.6 constant_dynamic-slice_fusion.4
  83.6 1.5 or_select_fusion.2
  85.2 7.3 %fusion.11 = f32[8,4,128,663]{2,3,1,0:T(8,128)} fusion(f32[8,4,128,663]{2,3,1,0:T(8,128)} %get-tuple-element.208, s32[]{:T(128)} %get-tuple-element.207, f32[4,1326]{1,0:T(4,128)S(1)} %dynamic-slice_bitcast_fusion.8, f32[4,663]{1,0:T(4,128)S(1)} %dynamic-slice_bitcast_fusion.9, f32[663,1326]{1,0:T(8,128)S(1)} %or_select_fusion.2, ...), kind=kOutput, calls=%fused_computation.5.clone.1 | convolution fusion | flops 924853184 | bytes 6298408 | tf_op jit(solution)/shard_map/while/body/eval_jaxpr/nij,nlj->nli/dot_general | solution.py:75
  92.5 1.6 constant_dynamic-slice_fusion.4
  94.1 1.5 or_select_fusion.2
  95.7 7.4 %fusion.11 = f32[8,4,128,663]{2,3,1,0:T(8,128)} fusion(f32[8,4,128,663]{2,3,1,0:T(8,128)} %get-tuple-element.208, s32[]{:T(128)} %get-tuple-element.207, f32[4,1326]{1,0:T(4,128)S(1)} %dynamic-slice_bitcast_fusion.8, f32[4,663]{1,0:T(4,128)S(1)} %dynamic-slice_bitcast_fusion.9, f32[663,1326]{1,0:T(8,128)S(1)} %or_select_fusion.2, ...), kind=kOutput, calls=%fused_computation.5.clone.1 | convolution fusion | flops 924853184 | bytes 6298408 | tf_op jit(solution)/shard_map/while/body/eval_jaxpr/nij,nlj->nli/dot_general | solution.py:75
  103.0 1.6 constant_dynamic-slice_fusion.4
  104.7 1.5 or_select_fusion.2
  106.2 7.3 %fusion.11 = f32[8,4,128,663]{2,3,1,0:T(8,128)} fusion(f32[8,4,128,663]{2,3,1,0:T(8,128)} %get-tuple-element.208, s32[]{:T(128)} %get-tuple-element.207, f32[4,1326]{1,0:T(4,128)S(1)} %dynamic-slice_bitcast_fusion.8, f32[4,663]{1,0:T(4,128)S(1)} %dynamic-slice_bitcast_fusion.9, f32[663,1326]{1,0:T(8,128)S(1)} %or_select_fusion.2, ...), kind=kOutput, calls=%fused_computation.5.clone.1 | convolution fusion | flops 924853184 | bytes 6298408 | tf_op jit(solution)/shard_map/while/body/eval_jaxpr/nij,nlj->nli/dot_general | solution.py:75
  113.5 12.0 %copy.23 = f32[8,4,128,663]{3,2,1,0:T(8,128)} copy(f32[8,4,128,663]{2,3,1,0:T(8,128)} %get-tuple-element.44) | data formatting | bytes 21725184 | tf_op jit(solution)/shard_map/while | solution.py:115
  125.6 0.1 copy.24
  125.7 0.2 copy.25
  125.9 16.8 %select_reduce_fusion = f32[32,2,8,663]{3,2,1,0:T(8,128)S(1)} fusion(f32[32,2,8,8,663]{4,3,2,1,0:T(8,128)} %bitcast.35, f32[32,2,8,8]{3,2,1,0:T(8,128)S(1)} %copy.25, pred[32,8]{1,0:T(8,128)(4,1)S(1)} %iota_compare_fusion), kind=kLoop, calls=%fused_computation.12 | loop fusion | flops 7807488 | bytes 12237056 | tf_op jit(solution)/shard_map/reduce_max | solution.py:83
  142.7 0.5 reduce_sum.27
  143.2 0.2 reshape.106
  143.4 0.8 fusion.5
  144.3 2.0 copy.26
  146.3 11.2 %all-to-all-start.1 = ((f32[64,4,1326]{2,1,0:T(4,128)}), f32[64,4,1326]{2,1,0:T(4,128)S(1)}, u32[]{:S(2)}, u32[]{:S(2)}) async-start(f32[64,4,1326]{2,1,0:T(4,128)} %copy.26), calls=%async_computation.1 | async-start | bytes 2883584 | tf_op jit(solution)/shard_map/all_to_all | solution.py:36
  157.6 0.6 dynamic_slice.38
  158.2 0.6 iota_compare_fusion.1
  158.8 21.0 %all-to-all-done.1 = f32[64,4,1326]{2,1,0:T(4,128)S(1)} async-done(((f32[64,4,1326]{2,1,0:T(4,128)}), f32[64,4,1326]{2,1,0:T(4,128)S(1)}, u32[]{:S(2)}, u32[]{:S(2)}) %all-to-all-start.1) | async-done | bytes 1357856 | tf_op jit(solution)/shard_map/all_to_all | solution.py:36
  179.8 0.3 reduce_sum.28
  180.3 1.3 multiply_reduce_fusion
  181.6 7.1 %psum.28 = f32[]{:T(128)} all-reduce(f32[]{:T(128)} %multiply_reduce_fusion), channel_id=1, replica_groups=mesh['node_0'=4,'node_1'=4,'node_2'=4,'hand'=2] {'node_0'}, use_global_device_ids=true, to_apply=%region_7.8 | all-reduce | flops 1 | bytes 8 | tf_op jit(solution)/shard_map/psum | solution.py:41
  188.7 7.0 %psum.29 = f32[]{:T(128)} all-reduce(f32[]{:T(128)} %psum.28), channel_id=1, replica_groups=mesh['node_0'=4,'node_1'=4,'node_2'=4,'hand'=2] {'node_1'}, use_global_device_ids=true, to_apply=%region_8.9 | all-reduce | flops 1 | bytes 8 | tf_op jit(solution)/shard_map/psum | solution.py:41
  195.7 7.4 %psum.30 = f32[]{:T(128)} all-reduce(f32[]{:T(128)} %psum.29), channel_id=1, replica_groups=mesh['node_0'=4,'node_1'=4,'node_2'=4,'hand'=2] {'node_2'}, use_global_device_ids=true, to_apply=%region_9.10 | all-reduce | flops 1 | bytes 8 | tf_op jit(solution)/shard_map/psum | solution.py:41
  203.0 10.3 %psum.31 = f32[]{:T(128)} all-reduce(f32[]{:T(128)} %psum.30), channel_id=1, replica_groups=mesh['node_0'=4,'node_1'=4,'node_2'=4,'hand'=2] {'hand'}, use_global_device_ids=true, to_apply=%region_10.11 | all-reduce | flops 1 | bytes 8 | tf_op jit(solution)/shard_map/psum | solution.py:41
  (62 shorter events, 1.0 us)
Async XLA Ops:
  11.2 9.3 %copy-start.3 = (s32[32,1326]{1,0:T(8,128)S(1)}, s32[32,1326]{1,0:T(8,128)}, u32[]{:S(2)}) copy-start(s32[32,1326]{1,0:T(8,128)} %param.14) | copy-start | bytes 509188
  11.2 9.5 %copy-start = (s32[32,1326]{1,0:T(8,128)S(1)}, s32[32,1326]{1,0:T(8,128)}, u32[]{:S(2)}) copy-start(s32[32,1326]{1,0:T(8,128)} %param.13) | copy-start | bytes 509188
  11.2 9.8 %copy-start.1 = (s32[1326]{0:T(1024)S(1)}, s32[1326]{0:T(1024)}, u32[]{:S(2)}) copy-start(s32[1326]{0:T(1024)} %constant.58.clone) | copy-start | bytes 15916
  11.2 9.8 %copy-start.2 = (s32[1326]{0:T(1024)S(1)}, s32[1326]{0:T(1024)}, u32[]{:S(2)}) copy-start(s32[1326]{0:T(1024)} %constant.59.clone) | copy-start | bytes 15916
  11.3 18.2 %all-to-all-start = ((bf16[2,32,128,663]{2,1,3,0:T(8,128)(2,1)}), bf16[2,32,128,663]{2,1,3,0:T(8,128)(2,1)}, u32[]{:S(2)}, u32[]{:S(2)}) async-start(bf16[2,32,128,663]{2,1,3,0:T(8,128)(2,1)} %pad_maximum_fusion), calls=%async_computation | async-start | bytes 21725184 | tf_op jit(solution)/shard_map/all_to_all | solution.py:18
  113.5 12.0 %copy-start.5 = (f32[32,128]{1,0:T(8,128)S(1)}, f32[32,128]{1,0:T(8,128)}, u32[]{:S(2)}) copy-start(f32[32,128]{1,0:T(8,128)} %param.15) | copy-start | bytes 49156
  113.5 12.3 %copy-start.7 = (s32[32]{0:T(128)S(1)}, s32[32]{0:T(128)}, u32[]{:S(2)}) copy-start(s32[32]{0:T(128)} %param.16) | copy-start | bytes 388
  125.6 17.8 %copy-start.6 = (s32[32]{0:T(128)S(1)}, s32[32]{0:T(128)}, u32[]{:S(2)}) copy-start(s32[32]{0:T(128)} %param.17) | copy-start | bytes 388
  125.9 31.6 %copy-start.8 = (s32[64]{0:T(128)S(1)}, s32[64]{0:T(128)}, u32[]{:S(2)}) copy-start(s32[64]{0:T(128)} %param.18) | copy-start | bytes 772
  146.3 33.5 %all-to-all-start.1 = ((f32[64,4,1326]{2,1,0:T(4,128)}), f32[64,4,1326]{2,1,0:T(4,128)S(1)}, u32[]{:S(2)}, u32[]{:S(2)}) async-start(f32[64,4,1326]{2,1,0:T(4,128)} %copy.26), calls=%async_computation.1 | async-start | bytes 2883584 | tf_op jit(solution)/shard_map/all_to_all | solution.py:36
  180.3 33.1 %copy-start.4 = (f32[1,2,663]{2,1,0:T(2,128)}, f32[1,2,663]{2,1,0:T(2,128)S(1)}, u32[]{:S(2)}) copy-start(f32[1,2,663]{2,1,0:T(2,128)S(1)} %reduce_max.22) | copy-start | bytes 15916
